TPU v7x, 8 devices: a whole 2x2x1 slice. The times are simulated.
8 devices in a mesh: dp: 2 (over z, y), fsdp: 4 (over x, core).
Axes of the slice: x: 2, y: 2, z: 1, core: 2. Of those that a mesh axis runs over, the one named last changes fastest.
Arguments:
- g_layer: float32 [8, 6, 256, 896], P(('dp', 'fsdp'))
- g_down: float32 [8, 256, 4864], P(('dp', 'fsdp'))
- g_norm: float32 [8, 4, 896], P(('dp', 'fsdp'))
- g_embed: float32 [8, 256, 896], P(('dp', 'fsdp'))
- layer_w: float32 [6, 256, 896], P(None, 'fsdp')
- layer_m: float32 [6, 256, 896], P(None, 'fsdp')
- layer_v: float32 [6, 256, 896], P(None, 'fsdp')
- down_w: float32 [256, 4864], P('fsdp')
- down_m: float32 [256, 4864], P('fsdp')
- down_v: float32 [256, 4864], P('fsdp')
- norm_w: float32 [4, 896], P(None, 'fsdp')
- norm_m: float32 [4, 896], P(None, 'fsdp')
- norm_v: float32 [4, 896], P(None, 'fsdp')
- embed_w: float32 [256, 896], P('fsdp')
- embed_m: float32 [256, 896], P('fsdp')
- embed_v: float32 [256, 896], P('fsdp')
Outputs:
- output 1: float32 [6, 256, 896], P(None, 'fsdp')
- output 2: float32 [6, 256, 896], P(None, 'fsdp')
- output 3: float32 [6, 256, 896], P(None, 'fsdp')
- output 4: bfloat16 [6, 256, 896], P(None, 'fsdp')
- output 5: float32 [256, 4864], P('fsdp')
- output 6: float32 [256, 4864], P('fsdp')
- output 7: float32 [256, 4864], P('fsdp')
- output 8: bfloat16 [256, 4864], P('fsdp')
- output 9: float32 [4, 896], P(None, 'fsdp')
- output 10: float32 [4, 896], P(None, 'fsdp')
- output 11: float32 [4, 896], P(None, 'fsdp')
- output 12: bfloat16 [4, 896], P(None, 'fsdp')
- output 13: float32 [256, 896], P('fsdp')
- output 14: float32 [256, 896], P('fsdp')
- output 15: float32 [256, 896], P('fsdp')
- output 16: bfloat16 [256, 896], P('fsdp')
All inputs are finite; a program needn't handle non-finite values.
Results may differ from a plain program's by a relative error of at most 0.001.
Values sent between devices are 32-bit elements.
A program may use at most 1 GiB of HBM per device.

v0:
```python
import jax
import jax.numpy as jnp
from jax import lax
from jax.experimental import pallas as pl
from jax.experimental.pallas import tpu as pltpu
from jax.sharding import PartitionSpec as P

ADAM_BETA1 = 0.9
ADAM_BETA2 = 0.95
ADAM_EPS = 1e-8
LEARN_RATE = 4e-4
WEIGHT_DECAY = 0.1
CLIP_EPS = 1e-6
OPT_STEP = 20
BIAS_ONE = 1.0 - ADAM_BETA1 ** OPT_STEP
BIAS_TWO = 1.0 - ADAM_BETA2 ** OPT_STEP

MESH = pl.DeviceIdType.MESH
LAYER, DOWN, NORM, EMBED = range(4)
DECAYS = (WEIGHT_DECAY, WEIGHT_DECAY, WEIGHT_DECAY, 0.0)
SHARES = ((6, 64, 896), (64, 4864), (4, 224), (64, 896))
WINDOWS = ((6, 64, 896), (64, 4864), (4, 384), (64, 896))
FIRST = slice(0, 8)

GROUPS = ((EMBED, FIRST), (EMBED, slice(8, 64)), (NORM, None), (DOWN, slice(0, 64)), (LAYER, None))


def plan():
    chunks = [(EMBED, (slice(r, r + 8),), int(r > 0)) for r in range(0, 64, 8)]
    chunks.append((NORM, (), 2))
    cuts = (0, 1024, 2048, 3072, 3968, 4864)
    chunks += [(DOWN, (slice(r, r + 8), slice(a, b)), 3) for r in range(0, 64, 8) for a, b in zip(cuts, cuts[1:])]
    chunks += [(LAYER, (l, slice(r, r + 8)), 4) for l in range(6) for r in range(0, 64, 8)]
    return chunks


CHUNKS = plan()
X_AHEAD, Y_BEHIND = 8, 5
X_RING, Y_RING = 2 * X_AHEAD + 2, 2 * Y_BEHIND + 2


def at(ref, index):
    return ref.at[tuple(pl.ds(i.start, i.stop - i.start) if isinstance(i, slice) else i for i in index)] if index else ref


def tile_sum(value):
    rows, columns = value.shape
    parts = [value[r:r + 8, c:c + 128] for r in range(0, rows, 8) for c in range(0, columns, 128)]
    while len(parts) > 1:
        parts = [a + b for a, b in zip(parts[::2], parts[1::2])] + parts[len(parts) // 2 * 2:]
    return parts[0]


def reduce_kernel(*refs):
    grads, states = refs[:4], refs[4:16]
    means, copies, clip = refs[16:20], refs[20:32], refs[32]
    far, near, x_in, y_in = (refs[33 + 4 * i:37 + 4 * i] for i in range(4))
    (first, norms, acc, first_sem, group_sem, state_sem, pair_send, x_send, y_send, x_recv, y_recv,
     norm_send, norm_recv) = refs[49:]

    dp, me = lax.axis_index("dp"), lax.axis_index("fsdp")
    partner = me + 1 - 2 * lax.rem(me, 2)
    across = lax.rem(me + 2, 4)
    diagonal = lax.rem(partner + 2, 4)
    other = 1 - dp
    peers = ((dp, across), (dp, diagonal), (dp, partner))
    held = (far, near)

    def share(array, fsdp, rows=None):
        ref = grads[array].at[0]
        if array == NORM:
            start = jnp.minimum((fsdp * 7) // 4, 4)
            return ref.at[:, pl.ds(pl.multiple_of(start * 128, 128), 384)]
        rows = rows or slice(0, 64)
        window = pl.ds(pl.multiple_of(fsdp * 64 + rows.start, 8), rows.stop - rows.start)
        return ref.at[:, window, :] if array == LAYER else ref.at[window, :]

    def slot(which, g, i):
        array, rows = GROUPS[g]
        ref = held[which][array].at[i]
        return ref if rows is None else ref.at[pl.ds(rows.start, rows.stop - rows.start), :]

    def load(which, g):
        array, rows = GROUPS[g]
        return pltpu.make_async_copy(
            share(array, (across, me)[which], rows), slot(which, g, 0), group_sem.at[which, g])

    def load_first(which):
        return pltpu.make_async_copy(
            share(EMBED, (diagonal, partner)[which], FIRST), first.at[which], first_sem)

    def pair(which, g):
        array, rows = GROUPS[g]
        return pltpu.make_async_remote_copy(
            src_ref=share(array, (diagonal, partner)[which], rows) if g else first.at[which],
            dst_ref=slot(which, g, 1), send_sem=pair_send, recv_sem=group_sem.at[which, g],
            device_id=(dp, partner), device_id_type=MESH)

    def over_x(c):
        array, index, _ = CHUNKS[c]
        return pltpu.make_async_remote_copy(
            src_ref=at(far[array].at[0], index), dst_ref=at(x_in[array], index),
            send_sem=x_send, recv_sem=x_recv.at[c % X_RING], device_id=(dp, across), device_id_type=MESH)

    def over_y(c):
        array, index, _ = CHUNKS[c]
        return pltpu.make_async_remote_copy(
            src_ref=at(near[array].at[0], index), dst_ref=at(y_in[array], index),
            send_sem=y_send, recv_sem=y_recv.at[c % Y_RING], device_id=(other, me), device_id_type=MESH)

    def norm_to(i):
        return pltpu.make_async_remote_copy(
            src_ref=norms.at[me], dst_ref=norms.at[me], send_sem=norm_send, recv_sem=norm_recv.at[i],
            device_id=peers[i], device_id_type=MESH)

    barrier = pltpu.get_barrier_semaphore()
    for device in ((other, me),) + peers:
        pl.semaphore_signal(barrier, inc=1, device_id=device, device_id_type=MESH)
    for which in (0, 1):
        load_first(which).start()
    for g in range(len(GROUPS)):
        for which in (0, 1):
            load(which, g).start()
    acc[...] = jnp.zeros_like(acc)
    pltpu.make_async_copy(first, first, first_sem).wait()
    pl.semaphore_wait(barrier, 4)
    for g in range(len(GROUPS)):
        for which in (0, 1):
            pair(which, g).start()
    for s, d in zip(states, copies):
        pltpu.make_async_copy(s, d, state_sem).start()

    ready = set()

    def need(which, g):
        if (which, g) not in ready:
            ready.add((which, g))
            array, rows = GROUPS[g]
            ref = held[which][array]
            if rows is not None:
                ref = ref.at[:, pl.ds(rows.start, rows.stop - rows.start), :]
            pltpu.make_async_copy(ref, ref, group_sem.at[which, g]).wait()

    def send_x(c):
        array, index, g = CHUNKS[c]
        need(0, g)
        ref = at(far[array].at[0], index)
        ref[...] = ref[...] + at(far[array].at[1], index)[...]
        over_x(c).start()

    def send_y(c):
        array, index, g = CHUNKS[c]
        need(1, g)
        over_x(c).wait_recv()
        ref = at(near[array].at[0], index)
        ref[...] = (ref[...] + at(near[array].at[1], index)[...]) + at(x_in[array], index)[...]
        over_y(c).start()

    def finish(c):
        array, index, _ = CHUNKS[c]
        over_y(c).wait_recv()
        mean = (at(near[array].at[0], index)[...] + at(y_in[array], index)[...]) * (1.0 / 8.0)
        if array == NORM:
            for f, skip in enumerate((0, 96, 64, 160)):
                @pl.when(me == f)
                def _():
                    mine = pltpu.roll(mean, (384 - skip) % 384, axis=1)
                    mine = jnp.where(lax.broadcasted_iota(jnp.int32, (4, 384), 1) < 224, mine, 0.0)
                    means[NORM][...] = mine[:, :224]
                    square = mine * mine
                    acc[0:4, :] = acc[0:4, :] + (square[:, :128] + square[:, 128:256])
        else:
            at(means[array], index)[...] = mean
            total = acc[...] + tile_sum(mean * mean)
            if c < len(CHUNKS) - 1:
                acc[...] = total
            else:
                norms[me] = total

    count = len(CHUNKS)
    for step in range(count + X_AHEAD + Y_BEHIND):
        if step < count:
            send_x(step)
        if 0 <= step - X_AHEAD < count:
            send_y(step - X_AHEAD)
        if 0 <= step - X_AHEAD - Y_BEHIND < count:
            finish(step - X_AHEAD - Y_BEHIND)
    for i in range(3):
        norm_to(i).start()

    for s, d in zip(states, copies):
        pltpu.make_async_copy(s, d, state_sem).wait()
    for array in range(4):
        for which in (0, 1):
            ref = held[which][array].at[0]
            pltpu.make_async_remote_copy(
                src_ref=ref, dst_ref=ref, send_sem=pair_send, recv_sem=norm_recv.at[0],
                device_id=(dp, partner), device_id_type=MESH).wait_send()
        pltpu.make_async_remote_copy(
            src_ref=far[array].at[0], dst_ref=x_in[array], send_sem=x_send, recv_sem=x_recv.at[0],
            device_id=(dp, across), device_id_type=MESH).wait_send()
        pltpu.make_async_remote_copy(
            src_ref=near[array].at[0], dst_ref=y_in[array], send_sem=y_send, recv_sem=y_recv.at[0],
            device_id=(other, me), device_id_type=MESH).wait_send()
    for i in range(3):
        norm_to(i).wait_send()
    for i in range(3):
        norm_to(i).wait_recv()
    total = (norms[0] + norms[1]) + (norms[2] + norms[3])
    total = jnp.sum(jnp.sum(total, axis=0, keepdims=True), axis=1, keepdims=True)
    norm = jnp.sqrt(jnp.broadcast_to(total, (8, 128)))
    clip[...] = jnp.minimum(1.0, 1.0 / (norm + CLIP_EPS))


def adamw(mean, master, exp_avg, exp_avg_sq, clip, decay):
    clipped = clip * mean
    avg_new = ADAM_BETA1 * exp_avg + (1.0 - ADAM_BETA1) * clipped
    sq_new = ADAM_BETA2 * exp_avg_sq + (1.0 - ADAM_BETA2) * clipped * clipped
    step_dir = (avg_new / BIAS_ONE) / (jnp.sqrt(sq_new / BIAS_TWO) + ADAM_EPS)
    master_new = master - LEARN_RATE * (step_dir + decay * master)
    return master_new, avg_new, sq_new, master_new.astype(jnp.bfloat16)


def update_kernel(*refs):
    means, states, clip_ref = refs[:4], refs[4:16], refs[16]
    outs, bufs, sem = refs[17:33], refs[33:49], refs[49]
    clip = clip_ref[...]

    def rows(array, index):
        ins = [means[array]] + list(states[3 * array:3 * array + 3])
        ins = [r[index] for r in ins]
        height, width = ins[0].shape
        scale = jnp.concatenate([clip[:height]] * -(-width // 128), axis=1)[:, :width]
        for o, value in zip(bufs[4 * array:4 * array + 4], adamw(*ins, scale, DECAYS[array])):
            o[index] = value

    def send(array, index):
        for k in range(4 * array, 4 * array + 4):
            pltpu.make_async_copy(at(bufs[k], index), at(outs[k], index), sem.at[k % SEMS]).start()

    for l in range(6):
        for r in range(0, 64, 8):
            rows(LAYER, (l, slice(r, r + 8)))
        send(LAYER, (l,))
    for r in range(0, 64, 8):
        rows(DOWN, (slice(r, r + 8),))
        send(DOWN, (slice(r, r + 8),))
    for r in range(0, 64, 8):
        rows(EMBED, (slice(r, r + 8),))
    send(EMBED, ())
    rows(NORM, (slice(0, 4),))
    send(NORM, ())
    for k in range(16):
        pltpu.make_async_copy(bufs[k], outs[k], sem.at[k % SEMS]).wait()


SEMS = 1


def solution(mesh):
    grad_four = P(("dp", "fsdp"), None, None, None)
    grad_three = P(("dp", "fsdp"), None, None)
    layer_spec = P(None, "fsdp", None)
    down_spec = P("fsdp", None)
    norm_spec = P(None, "fsdp")
    embed_spec = P("fsdp", None)
    any_spec = pl.BlockSpec(memory_space=pl.ANY)
    vmem_spec = pl.BlockSpec(memory_space=pltpu.VMEM)
    dma = pltpu.SemaphoreType.DMA
    f32 = jnp.float32

    def local_update(*args):
        state_shapes = [s for s in SHARES for _ in range(3)]
        results = pl.pallas_call(
            reduce_kernel,
            out_shape=tuple(pltpu.VMEM(s, f32) for s in list(SHARES) + state_shapes + [(8, 128)]),
            in_specs=[any_spec] * 16,
            out_specs=(vmem_spec,) * 17,
            scratch_shapes=[pltpu.VMEM(lead + s, f32) for lead in ((2,), (2,), (), ()) for s in WINDOWS] + [
                pltpu.VMEM((2, 8, 896), f32), pltpu.VMEM((4, 8, 128), f32), pltpu.VMEM((8, 128), f32),
                dma, dma((2, len(GROUPS))), dma, dma, dma, dma, dma((X_RING,)), dma((Y_RING,)), dma, dma((3,)),
            ],
            compiler_params=pltpu.CompilerParams(
                collective_id=0, has_side_effects=True, vmem_limit_bytes=24 * 1024 * 1024),
            name="reduce_grads",
        )(*(pltpu.with_memory_space_constraint(a, pltpu.HBM) for a in args))
        out_shapes = [(s, d) for s in SHARES for d in (f32, f32, f32, jnp.bfloat16)]
        return pl.pallas_call(
            update_kernel,
            out_shape=tuple(jax.ShapeDtypeStruct(s, d) for s, d in out_shapes),
            in_specs=[vmem_spec] * 17,
            out_specs=(any_spec,) * 16,
            scratch_shapes=[pltpu.VMEM(s, d) for s, d in out_shapes] + [dma((SEMS,))],
            compiler_params=pltpu.CompilerParams(vmem_limit_bytes=16 * 1024 * 1024),
            name="adamw_update",
        )(*(pltpu.with_memory_space_constraint(r, pltpu.VMEM) for r in results))

    in_specs = (grad_four, grad_three, grad_three, grad_three,
                layer_spec, layer_spec, layer_spec, down_spec, down_spec, down_spec,
                norm_spec, norm_spec, norm_spec, embed_spec, embed_spec, embed_spec)
    out_specs = (layer_spec,) * 4 + (down_spec,) * 4 + (norm_spec,) * 4 + (embed_spec,) * 4
    return jax.shard_map(local_update, mesh=mesh, in_specs=in_specs, out_specs=out_specs, check_vma=False)
```

profile of v0, /device:TPU:0, one launch (start us, length us, event | category | flops | bytes accessed | tf_op | source)
XLA Modules:
  0.0 79.6 jit_solution(10554977795046842291)
XLA Ops:
  0.7 75.0 %reduce_grads.1 = (f32[6,64,896]{2,1,0:T(8,128)S(1)}, f32[64,4864]{1,0:T(8,128)S(1)}, f32[4,224]{1,0:T(4,128)S(1)}, f32[64,896]{1,0:T(8,128)S(1)}, f32[6,64,896]...) custom-call(f32[1,6,256,896]{3,2,1,0:T(8,128)} %refs_0_.1, ...), custom_call_target="tpu_custom_call" | custom-call | tf_op jit(solution)/shard_map/reduce_grads/pallas_call | solution.py:274
  75.7 3.9 %adamw_update.1 = (f32[6,64,896]{2,1,0:T(8,128)}, f32[6,64,896]{2,1,0:T(8,128)}, f32[6,64,896]{2,1,0:T(8,128)}, bf16[6,64,896]{2,1,0:T(8,128)(2,1)}, f32[64,4864...) custom-call(f32[6,64,896]{2,1,0:T(8,128)S(1)} %get-tuple-element.33., ...), custom_call_target="tpu_custom_call" | custom-call | tf_op jit(solution)/shard_map/adamw_update/pallas_call | solution.py:288
where the time goes:
time: 79.7 us; the launch traced here: 79.6 us
  Pallas kernels  78.9 us (99%)
    pallas_call x1, Pallas kernels, local_update(): pl.pallas_call(reduce_kernel, out_shape=tuple((pltpu.VMEM(s, f32) for s i...  75 us
    pallas_call x1, Pallas kernels, local_update(): pl.pallas_call(update_kernel, out_shape=tuple((jax.ShapeDtypeStruct(s, d)...  3.94 us

commit v1 on v0

--- a/solution.py
+++ b/solution.py
@@ -22,15 +22,18 @@
 WINDOWS = ((6, 64, 896), (64, 4864), (4, 384), (64, 896))
 FIRST = slice(0, 8)
 
-GROUPS = ((EMBED, FIRST), (EMBED, slice(8, 64)), (NORM, None), (DOWN, slice(0, 64)), (LAYER, None))
+GROUPS = ([(EMBED, None, FIRST), (EMBED, None, slice(8, 64)), (NORM, None, None)]
+          + [(DOWN, None, slice(r, r + 8)) for r in range(0, 64, 8)] + [(LAYER, l, None) for l in range(6)])
+PAIR_AHEAD = 2
+PAIR_RING = 2 * PAIR_AHEAD
 
 
 def plan():
     chunks = [(EMBED, (slice(r, r + 8),), int(r > 0)) for r in range(0, 64, 8)]
     chunks.append((NORM, (), 2))
     cuts = (0, 1024, 2048, 3072, 3968, 4864)
-    chunks += [(DOWN, (slice(r, r + 8), slice(a, b)), 3) for r in range(0, 64, 8) for a, b in zip(cuts, cuts[1:])]
-    chunks += [(LAYER, (l, slice(r, r + 8)), 4) for l in range(6) for r in range(0, 64, 8)]
+    chunks += [(DOWN, (slice(r, r + 8), slice(a, b)), 3 + r // 8) for r in range(0, 64, 8) for a, b in zip(cuts, cuts[1:])]
+    chunks += [(LAYER, (l, slice(r, r + 8)), 11 + l) for l in range(6) for r in range(0, 64, 8)]
     return chunks
 
 
@@ -66,34 +69,35 @@
     peers = ((dp, across), (dp, diagonal), (dp, partner))
     held = (far, near)
 
-    def share(array, fsdp, rows=None):
+    def share(array, fsdp, layer=None, rows=None):
         ref = grads[array].at[0]
         if array == NORM:
             start = jnp.minimum((fsdp * 7) // 4, 4)
             return ref.at[:, pl.ds(pl.multiple_of(start * 128, 128), 384)]
         rows = rows or slice(0, 64)
         window = pl.ds(pl.multiple_of(fsdp * 64 + rows.start, 8), rows.stop - rows.start)
-        return ref.at[:, window, :] if array == LAYER else ref.at[window, :]
+        return ref.at[layer, window, :] if array == LAYER else ref.at[window, :]
 
     def slot(which, g, i):
-        array, rows = GROUPS[g]
-        ref = held[which][array].at[i]
-        return ref if rows is None else ref.at[pl.ds(rows.start, rows.stop - rows.start), :]
+        array, layer, rows = GROUPS[g]
+        ref = held[which][array]
+        lead = i if i is not None else slice(0, 2)
+        return at(ref, (lead, layer) if array == LAYER else (lead, rows) if rows is not None else (lead,))
 
     def load(which, g):
-        array, rows = GROUPS[g]
+        array, layer, rows = GROUPS[g]
         return pltpu.make_async_copy(
-            share(array, (across, me)[which], rows), slot(which, g, 0), group_sem.at[which, g])
+            share(array, (across, me)[which], layer, rows), slot(which, g, 0), group_sem.at[which, g % PAIR_RING])
 
     def load_first(which):
         return pltpu.make_async_copy(
-            share(EMBED, (diagonal, partner)[which], FIRST), first.at[which], first_sem)
+            share(EMBED, (diagonal, partner)[which], None, FIRST), first.at[which], first_sem)
 
     def pair(which, g):
-        array, rows = GROUPS[g]
+        array, layer, rows = GROUPS[g]
         return pltpu.make_async_remote_copy(
-            src_ref=share(array, (diagonal, partner)[which], rows) if g else first.at[which],
-            dst_ref=slot(which, g, 1), send_sem=pair_send, recv_sem=group_sem.at[which, g],
+            src_ref=share(array, (diagonal, partner)[which], layer, rows) if g else first.at[which],
+            dst_ref=slot(which, g, 1), send_sem=pair_send, recv_sem=group_sem.at[which, g % PAIR_RING],
             device_id=(dp, partner), device_id_type=MESH)
 
     def over_x(c):
@@ -118,13 +122,13 @@
         pl.semaphore_signal(barrier, inc=1, device_id=device, device_id_type=MESH)
     for which in (0, 1):
         load_first(which).start()
-    for g in range(len(GROUPS)):
+    for g in range(PAIR_AHEAD):
         for which in (0, 1):
             load(which, g).start()
     acc[...] = jnp.zeros_like(acc)
     pltpu.make_async_copy(first, first, first_sem).wait()
     pl.semaphore_wait(barrier, 4)
-    for g in range(len(GROUPS)):
+    for g in range(PAIR_AHEAD):
         for which in (0, 1):
             pair(which, g).start()
     for s, d in zip(states, copies):
@@ -135,11 +139,11 @@
     def need(which, g):
         if (which, g) not in ready:
             ready.add((which, g))
-            array, rows = GROUPS[g]
-            ref = held[which][array]
-            if rows is not None:
-                ref = ref.at[:, pl.ds(rows.start, rows.stop - rows.start), :]
-            pltpu.make_async_copy(ref, ref, group_sem.at[which, g]).wait()
+            ref = slot(which, g, None)
+            pltpu.make_async_copy(ref, ref, group_sem.at[which, g % PAIR_RING]).wait()
+            if g + PAIR_AHEAD < len(GROUPS):
+                pair(which, g + PAIR_AHEAD).start()
+                load(which, g + PAIR_AHEAD).start()
 
     def send_x(c):
         array, index, g = CHUNKS[c]
@@ -278,7 +282,7 @@
             out_specs=(vmem_spec,) * 17,
             scratch_shapes=[pltpu.VMEM(lead + s, f32) for lead in ((2,), (2,), (), ()) for s in WINDOWS] + [
                 pltpu.VMEM((2, 8, 896), f32), pltpu.VMEM((4, 8, 128), f32), pltpu.VMEM((8, 128), f32),
-                dma, dma((2, len(GROUPS))), dma, dma, dma, dma, dma((X_RING,)), dma((Y_RING,)), dma, dma((3,)),
+                dma, dma((2, PAIR_RING)), dma, dma, dma, dma, dma((X_RING,)), dma((Y_RING,)), dma, dma((3,)),
             ],
             compiler_params=pltpu.CompilerParams(
                 collective_id=0, has_side_effects=True, vmem_limit_bytes=24 * 1024 * 1024),

time: 79.7 us -> 78.9 us (0.990)
  no operation moved by 1% of the time
where the time goes in v1:
time: 78.9 us; the launch traced here: 78.8 us
  Pallas kernels  78.2 us (99%)
    pallas_call x1, Pallas kernels, local_update(): pl.pallas_call(reduce_kernel, out_shape=tuple((pltpu.VMEM(s, f32) for s i...  74.2 us
    pallas_call x1, Pallas kernels, local_update(): pl.pallas_call(update_kernel, out_shape=tuple((jax.ShapeDtypeStruct(s, d)...  3.94 us

profile of v1, /device:TPU:0, one launch (start us, length us, event | category | flops | bytes accessed | tf_op | source)
XLA Modules:
  0.0 78.8 jit_solution(16500453631255527496)
XLA Ops:
  0.7 74.2 %reduce_grads.1 = (f32[6,64,896]{2,1,0:T(8,128)S(1)}, f32[64,4864]{1,0:T(8,128)S(1)}, f32[4,224]{1,0:T(4,128)S(1)}, f32[64,896]{1,0:T(8,128)S(1)}, f32[6,64,896]...) custom-call(f32[1,6,256,896]{3,2,1,0:T(8,128)} %refs_0_.1, ...), custom_call_target="tpu_custom_call" | custom-call | tf_op jit(solution)/shard_map/reduce_grads/pallas_call | solution.py:278
  74.9 3.9 %adamw_update.1 = (f32[6,64,896]{2,1,0:T(8,128)}, f32[6,64,896]{2,1,0:T(8,128)}, f32[6,64,896]{2,1,0:T(8,128)}, bf16[6,64,896]{2,1,0:T(8,128)(2,1)}, f32[64,4864...) custom-call(f32[6,64,896]{2,1,0:T(8,128)S(1)} %get-tuple-element.33., ...), custom_call_target="tpu_custom_call" | custom-call | tf_op jit(solution)/shard_map/adamw_update/pallas_call | solution.py:292

commit v2 on v1

--- a/solution.py
+++ b/solution.py
@@ -20,26 +20,32 @@
 DECAYS = (WEIGHT_DECAY, WEIGHT_DECAY, WEIGHT_DECAY, 0.0)
 SHARES = ((6, 64, 896), (64, 4864), (4, 224), (64, 896))
 WINDOWS = ((6, 64, 896), (64, 4864), (4, 384), (64, 896))
-FIRST = slice(0, 8)
-
-GROUPS = ([(EMBED, None, FIRST), (EMBED, None, slice(8, 64)), (NORM, None, None)]
-          + [(DOWN, None, slice(r, r + 8)) for r in range(0, 64, 8)] + [(LAYER, l, None) for l in range(6)])
-PAIR_AHEAD = 2
+EARLY = 32
+HALF = EARLY // 2
+PIECES = range(0, HALF, 8)
+
+GROUPS = ([(EMBED, None, slice(EARLY, EARLY + 8)), (EMBED, None, slice(0, EARLY)), (EMBED, None, slice(EARLY + 8, 64)),
+           (LAYER, 0, None), (NORM, None, None)]
+          + [(DOWN, None, slice(r, r + 8)) for r in range(0, 64, 8)] + [(LAYER, l, None) for l in range(1, 6)])
+STAGED = 4
+PAIR_AHEAD = 4
 PAIR_RING = 2 * PAIR_AHEAD
 
 
 def plan():
-    chunks = [(EMBED, (slice(r, r + 8),), int(r > 0)) for r in range(0, 64, 8)]
-    chunks.append((NORM, (), 2))
+    chunks = [(EMBED, (slice(r, r + 8),), 0 if r == EARLY else 2) for r in range(EARLY, 64, 8)]
+    chunks += [(LAYER, (0, slice(r, r + 8)), 3) for r in range(0, 64, 8)]
+    chunks.append((NORM, (), 4))
     cuts = (0, 1024, 2048, 3072, 3968, 4864)
-    chunks += [(DOWN, (slice(r, r + 8), slice(a, b)), 3 + r // 8) for r in range(0, 64, 8) for a, b in zip(cuts, cuts[1:])]
-    chunks += [(LAYER, (l, slice(r, r + 8)), 11 + l) for l in range(6) for r in range(0, 64, 8)]
+    chunks += [(DOWN, (slice(r, r + 8), slice(a, b)), 5 + r // 8) for r in range(0, 64, 8) for a, b in zip(cuts, cuts[1:])]
+    chunks += [(LAYER, (l, slice(r, r + 8)), 12 + l) for l in range(1, 6) for r in range(0, 64, 8)]
     return chunks
 
 
 CHUNKS = plan()
 X_AHEAD, Y_BEHIND = 8, 5
 X_RING, Y_RING = 2 * X_AHEAD + 2, 2 * Y_BEHIND + 2
+EARLY_STEPS = {11: 0, 15: 1}
 
 
 def at(ref, index):
@@ -58,8 +64,8 @@
     grads, states = refs[:4], refs[4:16]
     means, copies, clip = refs[16:20], refs[20:32], refs[32]
     far, near, x_in, y_in = (refs[33 + 4 * i:37 + 4 * i] for i in range(4))
-    (first, norms, acc, first_sem, group_sem, state_sem, pair_send, x_send, y_send, x_recv, y_recv,
-     norm_send, norm_recv) = refs[49:]
+    (first, early_in, norms, acc, first_sem, group_sem, state_sem, pair_send, x_send, y_send, x_recv, y_recv,
+     early_recv, early_x, early_y, norm_send, norm_recv) = refs[49:]
 
     dp, me = lax.axis_index("dp"), lax.axis_index("fsdp")
     partner = me + 1 - 2 * lax.rem(me, 2)
@@ -89,14 +95,14 @@
         return pltpu.make_async_copy(
             share(array, (across, me)[which], layer, rows), slot(which, g, 0), group_sem.at[which, g % PAIR_RING])
 
-    def load_first(which):
+    def stage(which, i):
         return pltpu.make_async_copy(
-            share(EMBED, (diagonal, partner)[which], None, FIRST), first.at[which], first_sem)
+            share((EMBED, LAYER)[i], (diagonal, partner)[which], 0), first.at[i, which], first_sem.at[i])
 
     def pair(which, g):
         array, layer, rows = GROUPS[g]
         return pltpu.make_async_remote_copy(
-            src_ref=share(array, (diagonal, partner)[which], layer, rows) if g else first.at[which],
+            src_ref=share(array, (diagonal, partner)[which], layer, rows) if g >= STAGED else at(first, (int(array == LAYER), which) + (() if rows is None else (rows,))),
             dst_ref=slot(which, g, 1), send_sem=pair_send, recv_sem=group_sem.at[which, g % PAIR_RING],
             device_id=(dp, partner), device_id_type=MESH)
 
@@ -111,6 +117,25 @@
         return pltpu.make_async_remote_copy(
             src_ref=at(near[array].at[0], index), dst_ref=at(y_in[array], index),
             send_sem=y_send, recv_sem=y_recv.at[c % Y_RING], device_id=(other, me), device_id_type=MESH)
+
+    def half(owner, piece=None):
+        start, size = (0, HALF) if piece is None else (PIECES[piece], 8)
+        return pl.ds(pl.multiple_of(owner * HALF + start, 8), size)
+
+    def early(which):
+        return pltpu.make_async_remote_copy(
+            src_ref=held[which][EMBED].at[0, half(other), :], dst_ref=early_in.at[which],
+            send_sem=y_send, recv_sem=early_recv.at[which], device_id=(other, me), device_id_type=MESH)
+
+    def early_over_x(piece):
+        return pltpu.make_async_remote_copy(
+            src_ref=far[EMBED].at[0, half(dp, piece), :], dst_ref=x_in[EMBED].at[half(dp, piece), :],
+            send_sem=x_send, recv_sem=early_x.at[piece], device_id=(dp, across), device_id_type=MESH)
+
+    def early_over_y(piece, owner):
+        return pltpu.make_async_remote_copy(
+            src_ref=near[EMBED].at[0, half(owner, piece), :], dst_ref=y_in[EMBED].at[half(owner, piece), :],
+            send_sem=y_send, recv_sem=early_y.at[piece], device_id=(other, me), device_id_type=MESH)
 
     def norm_to(i):
         return pltpu.make_async_remote_copy(
@@ -120,17 +145,20 @@
     barrier = pltpu.get_barrier_semaphore()
     for device in ((other, me),) + peers:
         pl.semaphore_signal(barrier, inc=1, device_id=device, device_id_type=MESH)
-    for which in (0, 1):
-        load_first(which).start()
+    for i in (0, 1):
+        for which in (0, 1):
+            stage(which, i).start()
     for g in range(PAIR_AHEAD):
         for which in (0, 1):
             load(which, g).start()
     acc[...] = jnp.zeros_like(acc)
-    pltpu.make_async_copy(first, first, first_sem).wait()
+    pltpu.make_async_copy(first.at[0], first.at[0], first_sem.at[0]).wait()
     pl.semaphore_wait(barrier, 4)
-    for g in range(PAIR_AHEAD):
-        for which in (0, 1):
-            pair(which, g).start()
+    for which, g in ((0, 0), (0, 1), (0, 2), (1, 1), (1, 0), (1, 2)):
+        pair(which, g).start()
+    pltpu.make_async_copy(first.at[1], first.at[1], first_sem.at[1]).wait()
+    for which in (0, 1):
+        pair(which, 3).start()
     for s, d in zip(states, copies):
         pltpu.make_async_copy(s, d, state_sem).start()
 
@@ -181,14 +209,62 @@
             else:
                 norms[me] = total
 
+    def send_early(which):
+        need(which, 1)
+        ref = held[which][EMBED]
+        for owner in (other, dp):
+            ref[0, half(owner), :] = ref[0, half(owner), :] + ref[1, half(owner), :]
+            if owner is other:
+                early(which).start()
+
+    def send_early_x(piece):
+        if piece == 0:
+            early(0).wait_recv()
+        rows = half(dp, piece)
+        far[EMBED][0, rows, :] = far[EMBED][0, rows, :] + early_in[0, PIECES[piece]:PIECES[piece] + 8, :]
+        early_over_x(piece).start()
+
+    def send_early_y(piece):
+        if piece == 0:
+            early(1).wait_recv()
+        early_over_x(piece).wait_recv()
+        rows = half(dp, piece)
+        total = (near[EMBED][0, rows, :] + early_in[1, PIECES[piece]:PIECES[piece] + 8, :]) + x_in[EMBED][rows, :]
+        near[EMBED][0, rows, :] = total
+        means[EMBED][rows, :] = total * (1.0 / 8.0)
+        early_over_y(piece, dp).start()
+
+    def finish_early(piece):
+        early_over_y(piece, other).wait_recv()
+        rows = half(other, piece)
+        means[EMBED][rows, :] = y_in[EMBED][rows, :] * (1.0 / 8.0)
+        total = acc[...]
+        for owner in (0, 1):
+            mean = means[EMBED][half(owner, piece), :]
+            total = total + tile_sum(mean * mean)
+        acc[...] = total
+
     count = len(CHUNKS)
     for step in range(count + X_AHEAD + Y_BEHIND):
         if step < count:
             send_x(step)
+        if step == 0:
+            send_early(0)
+            send_early(1)
+
+            @pl.when(lax.rem(me, 2) == 1)
+            def _():
+                pl.delay(1800)
+        if step in EARLY_STEPS:
+            send_early_x(EARLY_STEPS[step])
         if 0 <= step - X_AHEAD < count:
             send_y(step - X_AHEAD)
+        if step - X_AHEAD in EARLY_STEPS:
+            send_early_y(EARLY_STEPS[step - X_AHEAD])
         if 0 <= step - X_AHEAD - Y_BEHIND < count:
             finish(step - X_AHEAD - Y_BEHIND)
+        if step - X_AHEAD - Y_BEHIND in EARLY_STEPS:
+            finish_early(EARLY_STEPS[step - X_AHEAD - Y_BEHIND])
     for i in range(3):
         norm_to(i).start()
 
@@ -200,12 +276,15 @@
             pltpu.make_async_remote_copy(
                 src_ref=ref, dst_ref=ref, send_sem=pair_send, recv_sem=norm_recv.at[0],
                 device_id=(dp, partner), device_id_type=MESH).wait_send()
+        rows = slice(HALF, 64) if array == EMBED else None
+        index = () if rows is None else (rows,)
         pltpu.make_async_remote_copy(
-            src_ref=far[array].at[0], dst_ref=x_in[array], send_sem=x_send, recv_sem=x_recv.at[0],
+            src_ref=at(far[array].at[0], index), dst_ref=at(x_in[array], index), send_sem=x_send, recv_sem=norm_recv.at[0],
             device_id=(dp, across), device_id_type=MESH).wait_send()
         pltpu.make_async_remote_copy(
-            src_ref=near[array].at[0], dst_ref=y_in[array], send_sem=y_send, recv_sem=y_recv.at[0],
+            src_ref=near[array].at[0], dst_ref=y_in[array], send_sem=y_send, recv_sem=norm_recv.at[0],
             device_id=(other, me), device_id_type=MESH).wait_send()
+    early(0).wait_send()
     for i in range(3):
         norm_to(i).wait_send()
     for i in range(3):
@@ -281,8 +360,9 @@
             in_specs=[any_spec] * 16,
             out_specs=(vmem_spec,) * 17,
             scratch_shapes=[pltpu.VMEM(lead + s, f32) for lead in ((2,), (2,), (), ()) for s in WINDOWS] + [
-                pltpu.VMEM((2, 8, 896), f32), pltpu.VMEM((4, 8, 128), f32), pltpu.VMEM((8, 128), f32),
-                dma, dma((2, PAIR_RING)), dma, dma, dma, dma, dma((X_RING,)), dma((Y_RING,)), dma, dma((3,)),
+                pltpu.VMEM((2, 2, 64, 896), f32), pltpu.VMEM((2, HALF, 896), f32), pltpu.VMEM((4, 8, 128), f32), pltpu.VMEM((8, 128), f32),
+                dma((2,)), dma((2, PAIR_RING)), dma, dma, dma, dma, dma((X_RING,)), dma((Y_RING,)),
+                dma((2,)), dma((len(PIECES),)), dma((len(PIECES),)), dma, dma((3,)),
             ],
             compiler_params=pltpu.CompilerParams(
                 collective_id=0, has_side_effects=True, vmem_limit_bytes=24 * 1024 * 1024),

time: 78.9 us -> 77.2 us (0.978)
  Pallas kernels: 78.2 us -> 76.4 us
    pallas_call x1, Pallas kernels: 74.2 us -> 72.5 us  [local_update(): pl.pallas_call(reduce_kernel, out_shape=tuple((pltpu.VMEM(s, f32) for s i...]
where the time goes in v2:
time: 77.2 us; the launch traced here: 77.1 us
  Pallas kernels  76.4 us (99%)
    pallas_call x1, Pallas kernels, local_update(): pl.pallas_call(reduce_kernel, out_shape=tuple((pltpu.VMEM(s, f32) for s i...  72.5 us
    pallas_call x1, Pallas kernels, local_update(): pl.pallas_call(update_kernel, out_shape=tuple((jax.ShapeDtypeStruct(s, d)...  3.94 us

profile of v2, /device:TPU:0, one launch (start us, length us, event | category | flops | bytes accessed | tf_op | source)
XLA Modules:
  0.0 77.1 jit_solution(2529280363207528646)
XLA Ops:
  0.7 72.5 %reduce_grads.1 = (f32[6,64,896]{2,1,0:T(8,128)S(1)}, f32[64,4864]{1,0:T(8,128)S(1)}, f32[4,224]{1,0:T(4,128)S(1)}, f32[64,896]{1,0:T(8,128)S(1)}, f32[6,64,896]...) custom-call(f32[1,6,256,896]{3,2,1,0:T(8,128)} %refs_0_.1, ...), custom_call_target="tpu_custom_call" | custom-call | tf_op jit(solution)/shard_map/reduce_grads/pallas_call | solution.py:357
  73.1 3.9 %adamw_update.1 = (f32[6,64,896]{2,1,0:T(8,128)}, f32[6,64,896]{2,1,0:T(8,128)}, f32[6,64,896]{2,1,0:T(8,128)}, bf16[6,64,896]{2,1,0:T(8,128)(2,1)}, f32[64,4864...) custom-call(f32[6,64,896]{2,1,0:T(8,128)S(1)} %get-tuple-element.33., ...), custom_call_target="tpu_custom_call" | custom-call | tf_op jit(solution)/shard_map/adamw_update/pallas_call | solution.py:372

commit v3 on v2

--- a/solution.py
+++ b/solution.py
@@ -43,7 +43,7 @@
 
 
 CHUNKS = plan()
-X_AHEAD, Y_BEHIND = 8, 5
+X_AHEAD, Y_BEHIND = 6, 5
 X_RING, Y_RING = 2 * X_AHEAD + 2, 2 * Y_BEHIND + 2
 EARLY_STEPS = {11: 0, 15: 1}
 
@@ -64,8 +64,8 @@
     grads, states = refs[:4], refs[4:16]
     means, copies, clip = refs[16:20], refs[20:32], refs[32]
     far, near, x_in, y_in = (refs[33 + 4 * i:37 + 4 * i] for i in range(4))
-    (first, early_in, norms, acc, first_sem, group_sem, state_sem, pair_send, x_send, y_send, x_recv, y_recv,
-     early_recv, early_x, early_y, norm_send, norm_recv) = refs[49:]
+    (first, raw_in, early_in, norms, acc, first_sem, group_sem, state_sem, send_sem, x_recv, y_recv,
+     early_recv, early_x, early_y, raw_recv, norm_recv) = refs[49:]
 
     dp, me = lax.axis_index("dp"), lax.axis_index("fsdp")
     partner = me + 1 - 2 * lax.rem(me, 2)
@@ -103,20 +103,25 @@
         array, layer, rows = GROUPS[g]
         return pltpu.make_async_remote_copy(
             src_ref=share(array, (diagonal, partner)[which], layer, rows) if g >= STAGED else at(first, (int(array == LAYER), which) + (() if rows is None else (rows,))),
-            dst_ref=slot(which, g, 1), send_sem=pair_send, recv_sem=group_sem.at[which, g % PAIR_RING],
+            dst_ref=slot(which, g, 1), send_sem=send_sem, recv_sem=group_sem.at[which, g % PAIR_RING],
             device_id=(dp, partner), device_id_type=MESH)
 
     def over_x(c):
         array, index, _ = CHUNKS[c]
         return pltpu.make_async_remote_copy(
             src_ref=at(far[array].at[0], index), dst_ref=at(x_in[array], index),
-            send_sem=x_send, recv_sem=x_recv.at[c % X_RING], device_id=(dp, across), device_id_type=MESH)
+            send_sem=send_sem, recv_sem=x_recv.at[c % X_RING], device_id=(dp, across), device_id_type=MESH)
+
+    def raw():
+        return pltpu.make_async_remote_copy(
+            src_ref=first.at[0, 0, pl.ds(EARLY, 8), :], dst_ref=raw_in, send_sem=send_sem, recv_sem=raw_recv,
+            device_id=(dp, diagonal), device_id_type=MESH)
 
     def over_y(c):
         array, index, _ = CHUNKS[c]
         return pltpu.make_async_remote_copy(
             src_ref=at(near[array].at[0], index), dst_ref=at(y_in[array], index),
-            send_sem=y_send, recv_sem=y_recv.at[c % Y_RING], device_id=(other, me), device_id_type=MESH)
+            send_sem=send_sem, recv_sem=y_recv.at[c % Y_RING], device_id=(other, me), device_id_type=MESH)
 
     def half(owner, piece=None):
         start, size = (0, HALF) if piece is None else (PIECES[piece], 8)
@@ -125,21 +130,21 @@
     def early(which):
         return pltpu.make_async_remote_copy(
             src_ref=held[which][EMBED].at[0, half(other), :], dst_ref=early_in.at[which],
-            send_sem=y_send, recv_sem=early_recv.at[which], device_id=(other, me), device_id_type=MESH)
+            send_sem=send_sem, recv_sem=early_recv.at[which], device_id=(other, me), device_id_type=MESH)
 
     def early_over_x(piece):
         return pltpu.make_async_remote_copy(
             src_ref=far[EMBED].at[0, half(dp, piece), :], dst_ref=x_in[EMBED].at[half(dp, piece), :],
-            send_sem=x_send, recv_sem=early_x.at[piece], device_id=(dp, across), device_id_type=MESH)
+            send_sem=send_sem, recv_sem=early_x.at[piece], device_id=(dp, across), device_id_type=MESH)
 
     def early_over_y(piece, owner):
         return pltpu.make_async_remote_copy(
             src_ref=near[EMBED].at[0, half(owner, piece), :], dst_ref=y_in[EMBED].at[half(owner, piece), :],
-            send_sem=y_send, recv_sem=early_y.at[piece], device_id=(other, me), device_id_type=MESH)
+            send_sem=send_sem, recv_sem=early_y.at[piece], device_id=(other, me), device_id_type=MESH)
 
     def norm_to(i):
         return pltpu.make_async_remote_copy(
-            src_ref=norms.at[me], dst_ref=norms.at[me], send_sem=norm_send, recv_sem=norm_recv.at[i],
+            src_ref=norms.at[me], dst_ref=norms.at[me], send_sem=send_sem, recv_sem=norm_recv.at[i],
             device_id=peers[i], device_id_type=MESH)
 
     barrier = pltpu.get_barrier_semaphore()
@@ -154,7 +159,21 @@
     acc[...] = jnp.zeros_like(acc)
     pltpu.make_async_copy(first.at[0], first.at[0], first_sem.at[0]).wait()
     pl.semaphore_wait(barrier, 4)
-    for which, g in ((0, 0), (0, 1), (0, 2), (1, 1), (1, 0), (1, 2)):
+    ready = set()
+
+    def need(which, g):
+        if (which, g) not in ready:
+            ready.add((which, g))
+            ref = slot(which, g, None if (which, g) != (0, 0) else 0)
+            pltpu.make_async_copy(ref, ref, group_sem.at[which, g % PAIR_RING]).wait()
+            if g + PAIR_AHEAD < len(GROUPS):
+                pair(which, g + PAIR_AHEAD).start()
+                load(which, g + PAIR_AHEAD).start()
+
+    need(0, 0)
+    over_x(0).start()
+    raw().start()
+    for which, g in ((0, 1), (0, 2), (1, 1), (1, 0), (1, 2)):
         pair(which, g).start()
     pltpu.make_async_copy(first.at[1], first.at[1], first_sem.at[1]).wait()
     for which in (0, 1):
@@ -162,18 +181,10 @@
     for s, d in zip(states, copies):
         pltpu.make_async_copy(s, d, state_sem).start()
 
-    ready = set()
-
-    def need(which, g):
-        if (which, g) not in ready:
-            ready.add((which, g))
-            ref = slot(which, g, None)
-            pltpu.make_async_copy(ref, ref, group_sem.at[which, g % PAIR_RING]).wait()
-            if g + PAIR_AHEAD < len(GROUPS):
-                pair(which, g + PAIR_AHEAD).start()
-                load(which, g + PAIR_AHEAD).start()
 
     def send_x(c):
+        if c == 0:
+            return
         array, index, g = CHUNKS[c]
         need(0, g)
         ref = at(far[array].at[0], index)
@@ -185,7 +196,11 @@
         need(1, g)
         over_x(c).wait_recv()
         ref = at(near[array].at[0], index)
-        ref[...] = (ref[...] + at(near[array].at[1], index)[...]) + at(x_in[array], index)[...]
+        total = (ref[...] + at(near[array].at[1], index)[...]) + at(x_in[array], index)[...]
+        if c == 0:
+            raw().wait_recv()
+            total = total + raw_in[...]
+        ref[...] = total
         over_y(c).start()
 
     def finish(c):
@@ -274,15 +289,15 @@
         for which in (0, 1):
             ref = held[which][array].at[0]
             pltpu.make_async_remote_copy(
-                src_ref=ref, dst_ref=ref, send_sem=pair_send, recv_sem=norm_recv.at[0],
+                src_ref=ref, dst_ref=ref, send_sem=send_sem, recv_sem=norm_recv.at[0],
                 device_id=(dp, partner), device_id_type=MESH).wait_send()
         rows = slice(HALF, 64) if array == EMBED else None
         index = () if rows is None else (rows,)
         pltpu.make_async_remote_copy(
-            src_ref=at(far[array].at[0], index), dst_ref=at(x_in[array], index), send_sem=x_send, recv_sem=norm_recv.at[0],
+            src_ref=at(far[array].at[0], index), dst_ref=at(x_in[array], index), send_sem=send_sem, recv_sem=norm_recv.at[0],
             device_id=(dp, across), device_id_type=MESH).wait_send()
         pltpu.make_async_remote_copy(
-            src_ref=near[array].at[0], dst_ref=y_in[array], send_sem=y_send, recv_sem=norm_recv.at[0],
+            src_ref=near[array].at[0], dst_ref=y_in[array], send_sem=send_sem, recv_sem=norm_recv.at[0],
             device_id=(other, me), device_id_type=MESH).wait_send()
     early(0).wait_send()
     for i in range(3):
@@ -321,7 +336,11 @@
         for k in range(4 * array, 4 * array + 4):
             pltpu.make_async_copy(at(bufs[k], index), at(outs[k], index), sem.at[k % SEMS]).start()
 
-    for l in range(6):
+    for r in range(0, 64, 8):
+        rows(LAYER, (0, slice(r, r + 8)))
+        if r % 16:
+            send(LAYER, (0, slice(r - 8, r + 8)))
+    for l in range(1, 6):
         for r in range(0, 64, 8):
             rows(LAYER, (l, slice(r, r + 8)))
         send(LAYER, (l,))
@@ -360,8 +379,8 @@
             in_specs=[any_spec] * 16,
             out_specs=(vmem_spec,) * 17,
             scratch_shapes=[pltpu.VMEM(lead + s, f32) for lead in ((2,), (2,), (), ()) for s in WINDOWS] + [
-                pltpu.VMEM((2, 2, 64, 896), f32), pltpu.VMEM((2, HALF, 896), f32), pltpu.VMEM((4, 8, 128), f32), pltpu.VMEM((8, 128), f32),
-                dma((2,)), dma((2, PAIR_RING)), dma, dma, dma, dma, dma((X_RING,)), dma((Y_RING,)),
+                pltpu.VMEM((2, 2, 64, 896), f32), pltpu.VMEM((8, 896), f32), pltpu.VMEM((2, HALF, 896), f32), pltpu.VMEM((4, 8, 128), f32), pltpu.VMEM((8, 128), f32),
+                dma((2,)), dma((2, PAIR_RING)), dma, dma, dma((X_RING,)), dma((Y_RING,)),
                 dma((2,)), dma((len(PIECES),)), dma((len(PIECES),)), dma, dma((3,)),
             ],
             compiler_params=pltpu.CompilerParams(

time: 77.2 us -> 77 us (level)
  no operation moved by 1% of the time
where the time goes in v3:
time: 77 us; the launch traced here: 76.9 us
  Pallas kernels  76.2 us (99%)
    pallas_call x1, Pallas kernels, local_update(): pl.pallas_call(reduce_kernel, out_shape=tuple((pltpu.VMEM(s, f32) for s i...  72.4 us
    pallas_call x1, Pallas kernels, local_update(): pl.pallas_call(update_kernel, out_shape=tuple((jax.ShapeDtypeStruct(s, d)...  3.86 us

profile of v3, /device:TPU:0, one launch (start us, length us, event | category | flops | bytes accessed | tf_op | source)
XLA Modules:
  0.0 76.9 jit_solution(16748005212410817684)
XLA Ops:
  0.7 72.4 %reduce_grads.1 = (f32[6,64,896]{2,1,0:T(8,128)S(1)}, f32[64,4864]{1,0:T(8,128)S(1)}, f32[4,224]{1,0:T(4,128)S(1)}, f32[64,896]{1,0:T(8,128)S(1)}, f32[6,64,896]...) custom-call(f32[1,6,256,896]{3,2,1,0:T(8,128)} %refs_0_.1, ...), custom_call_target="tpu_custom_call" | custom-call | tf_op jit(solution)/shard_map/reduce_grads/pallas_call | solution.py:376
  73.0 3.9 %adamw_update.1 = (f32[6,64,896]{2,1,0:T(8,128)}, f32[6,64,896]{2,1,0:T(8,128)}, f32[6,64,896]{2,1,0:T(8,128)}, bf16[6,64,896]{2,1,0:T(8,128)(2,1)}, f32[64,4864...) custom-call(f32[6,64,896]{2,1,0:T(8,128)S(1)} %get-tuple-element.33., ...), custom_call_target="tpu_custom_call" | custom-call | tf_op jit(solution)/shard_map/adamw_update/pallas_call | solution.py:391

commit v4 on v3

--- a/solution.py
+++ b/solution.py
@@ -144,7 +144,7 @@
 
     def norm_to(i):
         return pltpu.make_async_remote_copy(
-            src_ref=norms.at[me], dst_ref=norms.at[me], send_sem=send_sem, recv_sem=norm_recv.at[i],
+            src_ref=norms.at[me, pl.ds(0, 1), :], dst_ref=norms.at[me, pl.ds(0, 1), :], send_sem=send_sem, recv_sem=norm_recv.at[i],
             device_id=peers[i], device_id_type=MESH)
 
     barrier = pltpu.get_barrier_semaphore()
@@ -222,7 +222,7 @@
             if c < len(CHUNKS) - 1:
                 acc[...] = total
             else:
-                norms[me] = total
+                norms[me, 0:1, :] = jnp.sum(total, axis=0, keepdims=True)
 
     def send_early(which):
         need(which, 1)
@@ -304,8 +304,8 @@
         norm_to(i).wait_send()
     for i in range(3):
         norm_to(i).wait_recv()
-    total = (norms[0] + norms[1]) + (norms[2] + norms[3])
-    total = jnp.sum(jnp.sum(total, axis=0, keepdims=True), axis=1, keepdims=True)
+    rows = [norms[f, 0:1, :] for f in range(4)]
+    total = jnp.sum((rows[0] + rows[1]) + (rows[2] + rows[3]), axis=1, keepdims=True)
     norm = jnp.sqrt(jnp.broadcast_to(total, (8, 128)))
     clip[...] = jnp.minimum(1.0, 1.0 / (norm + CLIP_EPS))
 
@@ -338,12 +338,12 @@
 
     for r in range(0, 64, 8):
         rows(LAYER, (0, slice(r, r + 8)))
-        if r % 16:
-            send(LAYER, (0, slice(r - 8, r + 8)))
+        send(LAYER, (0, slice(r, r + 8)))
     for l in range(1, 6):
         for r in range(0, 64, 8):
             rows(LAYER, (l, slice(r, r + 8)))
-        send(LAYER, (l,))
+            if r % 32 == 24:
+                send(LAYER, (l, slice(r - 24, r + 8)))
     for r in range(0, 64, 8):
         rows(DOWN, (slice(r, r + 8),))
         send(DOWN, (slice(r, r + 8),))

time: 77 us -> 76.9 us (level)
  no operation moved by 1% of the time
where the time goes in v4:
time: 76.9 us; the launch traced here: 76.7 us
  Pallas kernels  76.1 us (99%)
    pallas_call x1, Pallas kernels, local_update(): pl.pallas_call(reduce_kernel, out_shape=tuple((pltpu.VMEM(s, f32) for s i...  72.3 us
    pallas_call x1, Pallas kernels, local_update(): pl.pallas_call(update_kernel, out_shape=tuple((jax.ShapeDtypeStruct(s, d)...  3.77 us

profile of v4, /device:TPU:0, one launch (start us, length us, event | category | flops | bytes accessed | tf_op | source)
XLA Modules:
  0.0 76.7 jit_solution(11225451353834861102)
XLA Ops:
  0.7 72.3 %reduce_grads.1 = (f32[6,64,896]{2,1,0:T(8,128)S(1)}, f32[64,4864]{1,0:T(8,128)S(1)}, f32[4,224]{1,0:T(4,128)S(1)}, f32[64,896]{1,0:T(8,128)S(1)}, f32[6,64,896]...) custom-call(f32[1,6,256,896]{3,2,1,0:T(8,128)} %refs_0_.1, ...), custom_call_target="tpu_custom_call" | custom-call | tf_op jit(solution)/shard_map/reduce_grads/pallas_call | solution.py:376
  73.0 3.8 %adamw_update.1 = (f32[6,64,896]{2,1,0:T(8,128)}, f32[6,64,896]{2,1,0:T(8,128)}, f32[6,64,896]{2,1,0:T(8,128)}, bf16[6,64,896]{2,1,0:T(8,128)(2,1)}, f32[64,4864...) custom-call(f32[6,64,896]{2,1,0:T(8,128)S(1)} %get-tuple-element.33., ...), custom_call_target="tpu_custom_call" | custom-call | tf_op jit(solution)/shard_map/adamw_update/pallas_call | solution.py:391

commit v5 on v4

--- a/solution.py
+++ b/solution.py
@@ -65,7 +65,7 @@
     means, copies, clip = refs[16:20], refs[20:32], refs[32]
     far, near, x_in, y_in = (refs[33 + 4 * i:37 + 4 * i] for i in range(4))
     (first, raw_in, early_in, norms, acc, first_sem, group_sem, state_sem, send_sem, x_recv, y_recv,
-     early_recv, early_x, early_y, raw_recv, norm_recv) = refs[49:]
+     early_recv, norm_recv) = refs[49:]
 
     dp, me = lax.axis_index("dp"), lax.axis_index("fsdp")
     partner = me + 1 - 2 * lax.rem(me, 2)
@@ -114,7 +114,7 @@
 
     def raw():
         return pltpu.make_async_remote_copy(
-            src_ref=first.at[0, 0, pl.ds(EARLY, 8), :], dst_ref=raw_in, send_sem=send_sem, recv_sem=raw_recv,
+            src_ref=first.at[0, 0, pl.ds(EARLY, 8), :], dst_ref=raw_in, send_sem=send_sem, recv_sem=norm_recv.at[2],
             device_id=(dp, diagonal), device_id_type=MESH)
 
     def over_y(c):
@@ -135,12 +135,12 @@
     def early_over_x(piece):
         return pltpu.make_async_remote_copy(
             src_ref=far[EMBED].at[0, half(dp, piece), :], dst_ref=x_in[EMBED].at[half(dp, piece), :],
-            send_sem=send_sem, recv_sem=early_x.at[piece], device_id=(dp, across), device_id_type=MESH)
+            send_sem=send_sem, recv_sem=norm_recv.at[piece], device_id=(dp, across), device_id_type=MESH)
 
     def early_over_y(piece, owner):
         return pltpu.make_async_remote_copy(
             src_ref=near[EMBED].at[0, half(owner, piece), :], dst_ref=y_in[EMBED].at[half(owner, piece), :],
-            send_sem=send_sem, recv_sem=early_y.at[piece], device_id=(other, me), device_id_type=MESH)
+            send_sem=send_sem, recv_sem=early_recv.at[piece], device_id=(other, me), device_id_type=MESH)
 
     def norm_to(i):
         return pltpu.make_async_remote_copy(
@@ -235,13 +235,12 @@
     def send_early_x(piece):
         if piece == 0:
             early(0).wait_recv()
+            early(1).wait_recv()
         rows = half(dp, piece)
         far[EMBED][0, rows, :] = far[EMBED][0, rows, :] + early_in[0, PIECES[piece]:PIECES[piece] + 8, :]
         early_over_x(piece).start()
 
     def send_early_y(piece):
-        if piece == 0:
-            early(1).wait_recv()
         early_over_x(piece).wait_recv()
         rows = half(dp, piece)
         total = (near[EMBED][0, rows, :] + early_in[1, PIECES[piece]:PIECES[piece] + 8, :]) + x_in[EMBED][rows, :]
@@ -381,7 +380,7 @@
             scratch_shapes=[pltpu.VMEM(lead + s, f32) for lead in ((2,), (2,), (), ()) for s in WINDOWS] + [
                 pltpu.VMEM((2, 2, 64, 896), f32), pltpu.VMEM((8, 896), f32), pltpu.VMEM((2, HALF, 896), f32), pltpu.VMEM((4, 8, 128), f32), pltpu.VMEM((8, 128), f32),
                 dma((2,)), dma((2, PAIR_RING)), dma, dma, dma((X_RING,)), dma((Y_RING,)),
-                dma((2,)), dma((len(PIECES),)), dma((len(PIECES),)), dma, dma((3,)),
+                dma((2,)), dma((3,)),
             ],
             compiler_params=pltpu.CompilerParams(
                 collective_id=0, has_side_effects=True, vmem_limit_bytes=24 * 1024 * 1024),

time: 76.9 us -> 76.8 us (level)
  no operation moved by 1% of the time
where the time goes in v5:
time: 76.8 us; the launch traced here: 76.7 us
  Pallas kernels  76 us (99%)
    pallas_call x1, Pallas kernels, local_update(): pl.pallas_call(reduce_kernel, out_shape=tuple((pltpu.VMEM(s, f32) for s i...  72.3 us
    pallas_call x1, Pallas kernels, local_update(): pl.pallas_call(update_kernel, out_shape=tuple((jax.ShapeDtypeStruct(s, d)...  3.77 us

profile of v5, /device:TPU:0, one launch (start us, length us, event | category | flops | bytes accessed | tf_op | source)
XLA Modules:
  0.0 76.7 jit_solution(4947924663506593358)
XLA Ops:
  0.7 72.3 %reduce_grads.1 = (f32[6,64,896]{2,1,0:T(8,128)S(1)}, f32[64,4864]{1,0:T(8,128)S(1)}, f32[4,224]{1,0:T(4,128)S(1)}, f32[64,896]{1,0:T(8,128)S(1)}, f32[6,64,896]...) custom-call(f32[1,6,256,896]{3,2,1,0:T(8,128)} %refs_0_.1, ...), custom_call_target="tpu_custom_call" | custom-call | tf_op jit(solution)/shard_map/reduce_grads/pallas_call | solution.py:375
  72.9 3.8 %adamw_update.1 = (f32[6,64,896]{2,1,0:T(8,128)}, f32[6,64,896]{2,1,0:T(8,128)}, f32[6,64,896]{2,1,0:T(8,128)}, bf16[6,64,896]{2,1,0:T(8,128)(2,1)}, f32[64,4864...) custom-call(f32[6,64,896]{2,1,0:T(8,128)S(1)} %get-tuple-element.33., ...), custom_call_target="tpu_custom_call" | custom-call | tf_op jit(solution)/shard_map/adamw_update/pallas_call | solution.py:390

commit v6 on v5

--- a/solution.py
+++ b/solution.py
@@ -64,7 +64,7 @@
     grads, states = refs[:4], refs[4:16]
     means, copies, clip = refs[16:20], refs[20:32], refs[32]
     far, near, x_in, y_in = (refs[33 + 4 * i:37 + 4 * i] for i in range(4))
-    (first, raw_in, early_in, norms, acc, first_sem, group_sem, state_sem, send_sem, x_recv, y_recv,
+    (first, raw_in, early_in, norms, acc, first_sem, group_sem, send_sem, x_recv, y_recv,
      early_recv, norm_recv) = refs[49:]
 
     dp, me = lax.axis_index("dp"), lax.axis_index("fsdp")
@@ -179,7 +179,7 @@
     for which in (0, 1):
         pair(which, 3).start()
     for s, d in zip(states, copies):
-        pltpu.make_async_copy(s, d, state_sem).start()
+        pltpu.make_async_copy(s, d, send_sem).start()
 
 
     def send_x(c):
@@ -283,7 +283,7 @@
         norm_to(i).start()
 
     for s, d in zip(states, copies):
-        pltpu.make_async_copy(s, d, state_sem).wait()
+        pltpu.make_async_copy(s, d, send_sem).wait()
     for array in range(4):
         for which in (0, 1):
             ref = held[which][array].at[0]
@@ -379,7 +379,7 @@
             out_specs=(vmem_spec,) * 17,
             scratch_shapes=[pltpu.VMEM(lead + s, f32) for lead in ((2,), (2,), (), ()) for s in WINDOWS] + [
                 pltpu.VMEM((2, 2, 64, 896), f32), pltpu.VMEM((8, 896), f32), pltpu.VMEM((2, HALF, 896), f32), pltpu.VMEM((4, 8, 128), f32), pltpu.VMEM((8, 128), f32),
-                dma((2,)), dma((2, PAIR_RING)), dma, dma, dma((X_RING,)), dma((Y_RING,)),
+                dma((2,)), dma((2, PAIR_RING)), dma, dma((X_RING,)), dma((Y_RING,)),
                 dma((2,)), dma((3,)),
             ],
             compiler_params=pltpu.CompilerParams(

time: 76.8 us -> 76.8 us (level)
  no operation moved by 1% of the time
where the time goes in v6:
time: 76.8 us; the launch traced here: 76.7 us
  Pallas kernels  76 us (99%)
    pallas_call x1, Pallas kernels, local_update(): pl.pallas_call(reduce_kernel, out_shape=tuple((pltpu.VMEM(s, f32) for s i...  72.3 us
    pallas_call x1, Pallas kernels, local_update(): pl.pallas_call(update_kernel, out_shape=tuple((jax.ShapeDtypeStruct(s, d)...  3.77 us

profile of v6, /device:TPU:0, one launch (start us, length us, event | category | flops | bytes accessed | tf_op | source)
XLA Modules:
  0.0 76.7 jit_solution(16498413609005134130)
XLA Ops:
  0.7 72.3 %reduce_grads.1 = (f32[6,64,896]{2,1,0:T(8,128)S(1)}, f32[64,4864]{1,0:T(8,128)S(1)}, f32[4,224]{1,0:T(4,128)S(1)}, f32[64,896]{1,0:T(8,128)S(1)}, f32[6,64,896]...) custom-call(f32[1,6,256,896]{3,2,1,0:T(8,128)} %refs_0_.1, ...), custom_call_target="tpu_custom_call" | custom-call | tf_op jit(solution)/shard_map/reduce_grads/pallas_call | solution.py:375
  72.9 3.8 %adamw_update.1 = (f32[6,64,896]{2,1,0:T(8,128)}, f32[6,64,896]{2,1,0:T(8,128)}, f32[6,64,896]{2,1,0:T(8,128)}, bf16[6,64,896]{2,1,0:T(8,128)(2,1)}, f32[64,4864...) custom-call(f32[6,64,896]{2,1,0:T(8,128)S(1)} %get-tuple-element.33., ...), custom_call_target="tpu_custom_call" | custom-call | tf_op jit(solution)/shard_map/adamw_update/pallas_call | solution.py:390
